TPU v7x, 128 devices: a whole 4x4x4 slice. The times are simulated.
128 devices in a mesh: row: 16 (over z, y_hi, core), col: 8 (over y_lo, x).
Axes of the slice: x: 4, y: 4 (y_hi: 2, y_lo: 2; y = y_hi * 2 + y_lo), z: 4, core: 2. Of those that a mesh axis runs over, the one named last changes fastest.
Arguments:
- left_prop: float32 [16, 8, 2, 512, 512], P('row', None, None, 'col'), may hold values from -0.1875 to 0.1875
- vertex: float32 [8, 2, 512, 512], P(None, None, ('row', 'col')), may hold values from -5 to 5
- right_prop: float32 [8, 16, 2, 512, 512], P(None, 'col', None, None, 'row'), may hold values from -0.1875 to 0.1875
- insertions: int32 [3], replicated, may hold values from 0 to 7
- window_start: int32 [2], replicated, may hold values from 0 to 255
Outputs:
- correlator: float32 [16, 16, 2, 512, 512], P('row', 'col')
Inputs may be any that keep to these rules, and one draw needn't show every extreme that they name: `insertions`: repeats may occur.
All inputs are finite; a program needn't handle non-finite values.
Results may differ from a plain program's by a relative error of at most 0.0001.
Values sent between devices are 32-bit elements; how exact they have to be, the bound alone decides.
No kernel may reach another device: no remote copies, remote signals or barrier semaphores. Data moves between devices by JAX's collectives and lax.ppermute only.
A program may use at most 128 MiB of HBM per device.

v0:
```python
import jax
import jax.numpy as jnp
from jax import lax
from jax.sharding import Mesh
from jax.sharding import PartitionSpec as P

NS = 8
LT = 256
ROW = ("row_0", "row_1", "row_2")
COL = ("col_0", "col_1")
ROW_COL = ("row_0", "row_1", "row_2", "col_0", "col_1")


def piece_ends(length, count):
    unit = 8 if length >= 8 * count else 1
    return [length // unit * k // count * unit for k in range(1, count)]


def all_blocks(x, axes, order):
    tiles = x[None]
    for k in order:
        tiles = lax.all_gather(tiles, axes[k], axis=0, tiled=True)
    held = [lax.axis_size(axes[k]) for k in reversed(order)]
    tiles = tiles.reshape(*held, *x.shape)
    turned = sorted(range(len(order)), key=lambda place: order[len(order) - 1 - place])
    return tiles.transpose(*turned, *range(len(order), tiles.ndim)).reshape(-1, *x.shape)


def in_order(tiles, dim):
    shape = list(tiles.shape[1:])
    shape[dim] *= tiles.shape[0]
    return jnp.moveaxis(tiles, 0, dim).reshape(shape)


def spread_gather(x, axes, dim):
    cut = max(range(max(1, x.ndim - 1)), key=lambda d: x.shape[d])
    count, finished = (len(axes), [])
    for leading, share in enumerate(jnp.split(x, piece_ends(x.shape[cut], count), axis=cut)):
        if share.size:
            order = [(leading - k) % count for k in range(count)]
            finished.append(all_blocks(share, axes, order))
    return in_order(jnp.concatenate(finished, axis=cut + 1), dim)


def complex_product(first, second):
    highest = lax.Precision.HIGHEST
    first_re, first_im = (first[..., 0, :, :], first[..., 1, :, :])
    second_re, second_im = (second[..., 0, :, :], second[..., 1, :, :])
    real_part = jnp.matmul(first_re, second_re, precision=highest) - jnp.matmul(
        first_im, second_im, precision=highest
    )
    imag_part = jnp.matmul(first_re, second_im, precision=highest) + jnp.matmul(
        first_im, second_re, precision=highest
    )
    return jnp.stack([real_part, imag_part], axis=-3)


def contract_with(left_operand, column_piece):
    summed = complex_product(left_operand[:, 0, None], column_piece[0][None])
    for which in range(1, column_piece.shape[0]):
        summed = summed + complex_product(left_operand[:, which, None], column_piece[which][None])
    return summed


def per_device(left_prop, vertex, right_prop, insertions, window_start):
    source_count = left_prop.shape[0]
    sink_count = right_prop.shape[1]
    source_slots = lax.axis_index(ROW) * source_count + jnp.arange(source_count, dtype=jnp.int32)
    sink_slots = lax.axis_index(COL) * sink_count + jnp.arange(sink_count, dtype=jnp.int32)
    slice_times = insertions * (LT // NS)
    source_times = (window_start[0] + source_slots) % LT
    sink_times = (window_start[1] + sink_slots) % LT
    left_sign = jnp.where(slice_times[None, :] < source_times[:, None], -1.0, 1.0).astype(
        jnp.float32
    )
    right_sign = jnp.where(sink_times[None, :] < slice_times[:, None], -1.0, 1.0).astype(
        jnp.float32
    )
    chosen_left = jnp.take(left_prop, insertions, axis=1) * left_sign[:, :, None, None, None]
    chosen_right = jnp.take(right_prop, insertions, axis=0) * right_sign[:, :, None, None, None]
    vertex_part = jnp.take(vertex, insertions, axis=0)
    vertex_full = spread_gather(vertex_part, ROW_COL, 2)
    left_full = lax.all_gather(chosen_left, COL, axis=3, tiled=True)
    vertex_right = complex_product(vertex_full[:, None], chosen_right)
    result = contract_with(left_full, lax.all_gather(vertex_right, ROW, axis=4, tiled=True))
    return result


def solution(mesh):
    finer = Mesh(mesh.devices.reshape(4, 2, 2, 2, 4), ("row_0", "row_1", "row_2", "col_0", "col_1"))
    return jax.shard_map(
        per_device,
        mesh=finer,
        in_specs=(
            P(ROW, None, None, COL, None),
            P(None, None, ROW_COL, None),
            P(None, COL, None, None, ROW),
            P(),
            P(),
        ),
        out_specs=P(ROW, COL, None, None, None),
        check_vma=False,
    )
```

profile of v0, /device:TPU:1, one launch (start us, length us, event | category | flops | bytes accessed | tf_op | source)
XLA Modules:
  0.0 401.7 jit_solution(11193293117327762396)
XLA Ops:
  9.6 5.5 %all-gather = f32[6,2,1,512]{3,1,2,0:T(2,128)S(1)} all-gather(f32[3,2,1,512]{3,1,2,0:T(2,128)S(1)} %copy.62), channel_id=2, replica_groups=mesh['row_0'=4,'row_1'=2,'row_2'=2,'col_0'=2,'col_1'=4] {'row_1'}, dimensions={0}, use_global_device_ids=true | all-gather | bytes 36864 | tf_op jit(solution)/shard_map/all_gather | solution.py:22
  15.1 10.3 %all_gather.68 = f32[8,3,2,1,512]{4,2,3,1,0:T(2,128)S(1)} all-gather(f32[2,3,2,1,512]{4,2,3,1,0:T(2,128)S(1)} %bitcast.186), channel_id=1, replica_groups=mesh['row_0'=4,'row_1'=2,'row_2'=2,'col_0'=2,'col_1'=4] {'row_0'}, dimensions={0}, use_global_device_ids=true | all-gather | bytes 122880 | tf_op jit(solution)/shard_map/all_gather | solution.py:22
  25.4 10.4 %all_gather.69 = f32[32,3,2,1,512]{4,2,3,1,0:T(2,128)S(1)} all-gather(f32[8,3,2,1,512]{4,2,3,1,0:T(2,128)S(1)} %all_gather.68), channel_id=1, replica_groups=mesh['row_0'=4,'row_1'=2,'row_2'=2,'col_0'=2,'col_1'=4] {'col_1'}, dimensions={0}, use_global_device_ids=true | all-gather | bytes 491520 | tf_op jit(solution)/shard_map/all_gather | solution.py:22
  35.9 7.4 %all_gather.70 = f32[64,3,2,1,512]{4,2,3,1,0:T(2,128)} all-gather(f32[32,3,2,1,512]{4,2,3,1,0:T(2,128)S(1)} %all_gather.69), channel_id=1, replica_groups=mesh['row_0'=4,'row_1'=2,'row_2'=2,'col_0'=2,'col_1'=4] {'col_0'}, dimensions={0}, use_global_device_ids=true | all-gather | bytes 1179648 | tf_op jit(solution)/shard_map/all_gather | solution.py:22
  43.4 9.9 %all-gather.1 = f32[6,2,1,512]{3,1,2,0:T(2,128)S(1)} all-gather(f32[3,2,1,512]{3,1,2,0:T(2,128)S(1)} %copy.65), channel_id=3, replica_groups=mesh['row_0'=4,'row_1'=2,'row_2'=2,'col_0'=2,'col_1'=4] {'row_2'}, dimensions={0}, use_global_device_ids=true | all-gather | bytes 36864 | tf_op jit(solution)/shard_map/all_gather | solution.py:22
  53.3 4.8 %all_gather.73 = f32[4,3,2,1,512]{4,2,3,1,0:T(2,128)S(1)} all-gather(f32[2,3,2,1,512]{4,2,3,1,0:T(2,128)S(1)} %bitcast.184), channel_id=1, replica_groups=mesh['row_0'=4,'row_1'=2,'row_2'=2,'col_0'=2,'col_1'=4] {'row_1'}, dimensions={0}, use_global_device_ids=true | all-gather | bytes 73728 | tf_op jit(solution)/shard_map/all_gather | solution.py:22
  58.1 9.2 %all_gather.74 = f32[16,3,2,1,512]{4,2,3,1,0:T(2,128)S(1)} all-gather(f32[4,3,2,1,512]{4,2,3,1,0:T(2,128)S(1)} %all_gather.73), channel_id=1, replica_groups=mesh['row_0'=4,'row_1'=2,'row_2'=2,'col_0'=2,'col_1'=4] {'row_0'}, dimensions={0}, use_global_device_ids=true | all-gather | bytes 245760 | tf_op jit(solution)/shard_map/all_gather | solution.py:22
  67.4 11.5 %all_gather.75 = f32[64,3,2,1,512]{4,2,3,1,0:T(2,128)} all-gather(f32[16,3,2,1,512]{4,2,3,1,0:T(2,128)S(1)} %all_gather.74), channel_id=1, replica_groups=mesh['row_0'=4,'row_1'=2,'row_2'=2,'col_0'=2,'col_1'=4] {'col_1'}, dimensions={0}, use_global_device_ids=true | all-gather | bytes 983040 | tf_op jit(solution)/shard_map/all_gather | solution.py:22
  82.5 9.5 %all_gather.78 = f32[4,3,2,1,512]{4,2,3,1,0:T(2,128)S(1)} all-gather(f32[2,3,2,1,512]{4,2,3,1,0:T(2,128)S(1)} %bitcast.185), channel_id=1, replica_groups=mesh['row_0'=4,'row_1'=2,'row_2'=2,'col_0'=2,'col_1'=4] {'row_2'}, dimensions={0}, use_global_device_ids=true | all-gather | bytes 73728 | tf_op jit(solution)/shard_map/all_gather | solution.py:22
  92.1 5.1 %all_gather.79 = f32[8,3,2,1,512]{4,2,3,1,0:T(2,128)S(1)} all-gather(f32[4,3,2,1,512]{4,2,3,1,0:T(2,128)S(1)} %all_gather.78), channel_id=1, replica_groups=mesh['row_0'=4,'row_1'=2,'row_2'=2,'col_0'=2,'col_1'=4] {'row_1'}, dimensions={0}, use_global_device_ids=true | all-gather | bytes 147456 | tf_op jit(solution)/shard_map/all_gather | solution.py:22
  97.2 10.7 %all_gather.80 = f32[32,3,2,1,512]{4,2,3,1,0:T(2,128)} all-gather(f32[8,3,2,1,512]{4,2,3,1,0:T(2,128)S(1)} %all_gather.79), channel_id=1, replica_groups=mesh['row_0'=4,'row_1'=2,'row_2'=2,'col_0'=2,'col_1'=4] {'row_0'}, dimensions={0}, use_global_device_ids=true | all-gather | bytes 491520 | tf_op jit(solution)/shard_map/all_gather | solution.py:22
  108.0 9.1 %all-gather.3 = f32[12,2,1,512]{3,1,2,0:T(2,128)S(1)} all-gather(f32[3,2,1,512]{3,1,2,0:T(2,128)S(1)} %copy.71), channel_id=5, replica_groups=mesh['row_0'=4,'row_1'=2,'row_2'=2,'col_0'=2,'col_1'=4] {'col_1'}, dimensions={0}, use_global_device_ids=true | all-gather | bytes 61440 | tf_op jit(solution)/shard_map/all_gather | solution.py:22
  117.2 3.9 all_gather.83
  121.1 9.2 %all_gather.84 = f32[16,3,2,1,512]{4,3,0,1,2:T(1,128)S(1)} all-gather(f32[8,3,2,1,512]{4,3,0,1,2:T(1,128)S(1)} %all_gather.83), channel_id=1, replica_groups=mesh['row_0'=4,'row_1'=2,'row_2'=2,'col_0'=2,'col_1'=4] {'row_2'}, dimensions={0}, use_global_device_ids=true | all-gather | bytes 294912 | tf_op jit(solution)/shard_map/all_gather | solution.py:22
  130.3 9.6 %all_gather.85 = f32[32,3,2,1,512]{4,3,0,1,2:T(1,128)} all-gather(f32[16,3,2,1,512]{4,3,0,1,2:T(1,128)S(1)} %all_gather.84), channel_id=1, replica_groups=mesh['row_0'=4,'row_1'=2,'row_2'=2,'col_0'=2,'col_1'=4] {'row_1'}, dimensions={0}, use_global_device_ids=true | all-gather | bytes 589824 | tf_op jit(solution)/shard_map/all_gather | solution.py:22
  149.7 3.7 reshape.208
  157.0 4.3 %reshape.210 = f32[128,3,2,1,512]{4,3,0,1,2:T(1,128)} reshape(f32[4,2,2,2,4,3,2,1,512]{8,4,3,2,1,0,5,6,7:T(4,128)} %copy.67) | data formatting | bytes 3145728 | tf_op jit(solution)/shard_map/reshape | solution.py:26
  164.9 4.2 %reshape.212 = f32[128,3,2,1,512]{4,3,0,1,2:T(1,128)} reshape(f32[4,2,2,2,4,3,2,1,512]{8,4,3,2,1,0,5,6,7:T(4,128)} %copy.70) | data formatting | bytes 3145728 | tf_op jit(solution)/shard_map/reshape | solution.py:26
  169.1 3.9 all-gather.19.cloned.1.call-done
  173.0 8.6 %maximum_bitcast_fusion = f32[3,2,128,4,512]{4,3,2,0,1:T(4,128)} fusion(f32[128,3,2,1,512]{4,3,0,1,2:T(1,128)} %all-gather.19.cloned.1.call-done, f32[128,3,2,1,512]{4,3,0,1,2:T(1,128)} %reshape.212, f32[128,3,2,1,512]{4,3,0,1,2:T(1,128)} %reshape.210, f32[128,3,2,1,512]{4,3,0,1,2:T(1,128)S(1)} %reshape.208), kind=kLoop, calls=%fused_computation.3 | loop fusion | flops 4718592 | bytes 12582912 | tf_op jit(solution)/shard_map/transpose | solution.py:32
  181.6 8.2 %broadcast_in_dim_reshape.3 = f32[3,1,2,512,512]{4,3,0,2,1:T(8,128)} reshape(f32[3,2,128,4,512]{4,3,2,0,1:T(4,128)} %maximum_bitcast_fusion) | data formatting | bytes 12582912 | tf_op jit(solution)/shard_map/broadcast_in_dim;reshape | solution.py:84
  189.8 5.2 %fusion.1 = f32[3,512,64]{1,2,0:S(1)} fusion(f32[3,512,64]{1,2,0:T(8,128)S(1)} %bitcast.174, f32[3,1,2,512,512]{4,3,0,2,1:T(8,128)} %broadcast_in_dim_reshape.3), kind=kOutput, calls=%fused_computation.8 | convolution fusion | flops 603979776 | bytes 3932160
  195.1 5.1 %fusion.4 = f32[3,512,64]{1,2,0:S(1)} fusion(f32[3,512,64]{1,2,0:T(8,128)S(1)} %bitcast.175, f32[3,1,2,512,512]{4,3,0,2,1:T(8,128)} %broadcast_in_dim_reshape.3), kind=kOutput, calls=%fused_computation.11 | convolution fusion | flops 603979776 | bytes 3932160
  207.6 38.9 %all-gather.11.cloned.1.call-done = f32[1,3,2,512,512]{4,3,2,1,0:T(8,128)} async-done(((f32[1,3,2,64,512]{4,3,2,1,0:T(8,128)}), f32[1,3,2,512,512]{4,3,2,1,0:T(8,128)}) %all-gather.11.cloned.1.call-update) | async-done | bytes 6291472 | tf_op jit(solution)/shard_map/all_gather | solution.py:83
  246.5 92.3 %all-gather.21.cloned.1.call-done = f32[3,2,2,512,512]{3,4,1,0,2:T(8,128)} async-done(((f32[3,2,2,512,32]{3,4,1,0,2:T(8,128)}), f32[3,2,2,512,512]{3,4,1,0,2:T(8,128)}) %all-gather.21.cloned.1.call-update) | async-done | bytes 12582928 | tf_op jit(solution)/shard_map/all_gather | solution.py:85
  338.9 5.8 %fusion.13 = f32[512,2,512]{2,0,1:T(8,128)S(1)} fusion(f32[3,2,2,512,512]{3,4,1,0,2:T(8,128)} %all-gather.21.cloned.1.call-done, f32[1,3,2,512,512]{4,3,2,1,0:T(8,128)} %all-gather.11.cloned.1.call-done), kind=kOutput, calls=%fused_computation.32 | convolution fusion | flops 3221225472 | bytes 5242880 | tf_op jit(solution)/shard_map/dot_general | solution.py:52
  344.7 5.5 %fusion.9 = f32[512,2,512]{2,0,1:T(8,128)S(1)} fusion(f32[3,2,2,512,512]{3,4,1,0,2:T(8,128)} %all-gather.21.cloned.1.call-done, f32[1,3,2,512,512]{4,3,2,1,0:T(8,128)} %all-gather.11.cloned.1.call-done), kind=kOutput, calls=%fused_computation.28 | convolution fusion | flops 3221225472 | bytes 5242880 | tf_op jit(solution)/shard_map/dot_general | solution.py:52
  350.2 5.6 %fusion.5 = f32[512,2,512]{2,0,1:T(8,128)S(1)} fusion(f32[3,2,2,512,512]{3,4,1,0,2:T(8,128)} %all-gather.21.cloned.1.call-done, f32[1,3,2,512,512]{4,3,2,1,0:T(8,128)} %all-gather.11.cloned.1.call-done), kind=kOutput, calls=%fused_computation.24 | convolution fusion | flops 3221225472 | bytes 5242880 | tf_op jit(solution)/shard_map/dot_general | solution.py:52
  355.9 5.1 %fusion.14 = f32[512,2,512]{2,0,1:T(8,128)S(1)} fusion(f32[3,2,2,512,512]{3,4,1,0,2:T(8,128)S(1)} %copy-done.3, f32[1,3,2,512,512]{4,3,2,1,0:T(8,128)} %all-gather.11.cloned.1.call-done), kind=kOutput, calls=%fused_computation.33 | convolution fusion | flops 3221225472 | bytes 5242880 | tf_op jit(solution)/shard_map/dot_general | solution.py:49
  371.7 4.0 %add_bitcast_fusion.1 = f32[1,2,1,512,512]{4,3,1,2,0:T(8,128)S(1)} fusion(f32[512,2,512]{2,0,1:T(8,128)S(1)} %fusion.9, f32[3,2,2,512,512]{3,4,1,0,2:T(8,128)S(1)} %copy-done.3, f32[1,3,2,512,512]{4,3,2,1,0:T(8,128)S(1)} %copy-done.4), kind=kOutput, calls=%fused_computation.20 | convolution fusion | flops 3221749760 | bytes 7340032 | tf_op jit(solution)/shard_map/dot_general | solution.py:52
  383.0 3.8 subtract_bitcast_fusion.1
  386.8 3.7 subtract_bitcast_fusion.2
  (64 shorter events, 52.6 us)
Async XLA Ops:
  6.5 134.7 %copy-start = (f32[1,8,2,64,512]{4,3,2,1,0:T(8,128)S(1)}, f32[1,8,2,64,512]{4,3,2,1,0:T(8,128)}, u32[]{:S(2)}) copy-start(f32[1,8,2,64,512]{4,3,2,1,0:T(8,128)} %param.5) | copy-start | bytes 6291460
  6.5 139.6 %all-gather.13.cloned.1.call-start = ((), (), s32[]{:S(2)}) async-start(), calls=%async_computation.1 | async-start | bytes 2359296 | tf_op jit(solution)/shard_map/all_gather | solution.py:22
  43.3 96.7 %copy-start.5 = (s32[2]{0:T(128)S(1)}, s32[2]{0:T(128)}, u32[]{:S(2)}) copy-start(s32[2]{0:T(128)} %param.9) | copy-start | bytes 28
  43.3 110.1 %all-gather.15.cloned.1.call-start = ((), (), s32[]{:S(2)}) async-start(), calls=%async_computation.2 | async-start | bytes 2359296 | tf_op jit(solution)/shard_map/all_gather | solution.py:22
  67.4 74.5 %copy-start.6 = (s32[3]{0:T(128)S(1)}, s32[3]{0:T(128)}, u32[]{:S(2)}) copy-start(s32[3]{0:T(128)} %param.8) | copy-start | bytes 40
  78.8 82.4 %all-gather.17.cloned.1.call-start = ((), (), s32[]{:S(2)}) async-start(), calls=%async_computation.3 | async-start | bytes 1966080 | tf_op jit(solution)/shard_map/all_gather | solution.py:22
  107.9 65.1 %all-gather.19.cloned.1.call-start = ((), (), s32[]{:S(2)}) async-start(), calls=%async_computation.4 | async-start | bytes 1966080 | tf_op jit(solution)/shard_map/all_gather | solution.py:22
  139.9 106.6 %all-gather.11.cloned.1.call-start = ((), (), s32[]{:S(2)}) async-start(), calls=%async_computation | async-start | bytes 7077888 | tf_op jit(solution)/shard_map/all_gather | solution.py:83
  142.9 195.9 %all-gather.21.cloned.1.call-start = ((), (), s32[]{:S(2)}) async-start(), calls=%async_computation.5 | async-start | bytes 13369344 | tf_op jit(solution)/shard_map/all_gather | solution.py:85
  189.8 10.3 %copy-start.2 = (f32[3,1,2,512,512]{4,3,0,2,1:T(8,128)S(1)}, f32[3,1,2,512,512]{4,3,0,2,1:T(8,128)}, u32[]{:S(2)}) copy-start(f32[3,1,2,512,512]{4,3,0,2,1:T(8,128)} %broadcast_in_dim_reshape.3) | copy-start | bytes 18874372
  338.9 17.0 %copy-start.3 = (f32[3,2,2,512,512]{3,4,1,0,2:T(8,128)S(1)}, f32[3,2,2,512,512]{3,4,1,0,2:T(8,128)}, u32[]{:S(2)}) copy-start(f32[3,2,2,512,512]{3,4,1,0,2:T(8,128)} %all-gather.21.cloned.1.call-done) | copy-start | bytes 37748740
  350.2 10.7 %copy-start.4 = (f32[1,3,2,512,512]{4,3,2,1,0:T(8,128)S(1)}, f32[1,3,2,512,512]{4,3,2,1,0:T(8,128)}, u32[]{:S(2)}) copy-start(f32[1,3,2,512,512]{4,3,2,1,0:T(8,128)} %all-gather.11.cloned.1.call-done) | copy-start | bytes 18874372
  390.6 4.1 %copy-start.1 = (f32[1,8,2,64,512]{4,3,2,1,0:T(8,128)S(1)}, f32[1,8,2,64,512]{4,3,2,1,0:T(8,128)}, u32[]{:S(2)}) copy-start(f32[1,8,2,64,512]{4,3,2,1,0:T(8,128)} %param.5) | copy-start | bytes 6291460
Sparse Core Ops, SparseCore 0:
  43.4 21.2 all-gather.12
  79.0 36.6 all-gather.14
  117.4 27.3 all-gather.16
  146.3 26.6 all-gather.18
  174.5 71.9 all-gather.10
  248.8 89.9 all-gather.20
where the time goes:
time: 406 us; the launch traced here: 402 us
  waiting for transfers between devices  135 us (33%)
  blocking collectives  130 us (32%)
  matrix products  68.2 us (17%)
  local copies, waits for them, and re-layouts  38.6 us (10%)
  other arithmetic  14.7 us (4%)
  between operations  14.7 us (4%)
    all_gather x16, blocking collectives, all_blocks(): tiles = lax.all_gather(tiles, axes[k], axis=0, tiled=True)  130 us
    all_gather x1, waiting for transfers between devices, per_device(): lax.all_gather(vertex_right, ROW, axis=4, tiled=True)  92.3 us
    all_gather x1, waiting for transfers between devices, per_device(): left_full = lax.all_gather(chosen_left, COL, axis=3, tiled=True)  38.9 us
    dot_general x3, matrix products, complex_product(): jnp.matmul(first_im, second_re, precision=highest)  17 us
    unnamed x4, matrix products  16.6 us
    reshape x3, local copies, waits for them, and re-layouts, all_blocks(): tiles.transpose(*turned, *range(len(order), tiles.ndim))  12.2 us
    dot_general x3, matrix products, complex_product(): jnp.matmul(first_re, second_re, precision=highest)  12.2 us
    dot_general x3, matrix products, complex_product(): jnp.matmul(first_re, second_im, precision=highest)  11.3 us
  transfers between devices with their start and end apart: 6, of which 3 were waited for; matrix products, arithmetic and copies ran while one was open for 16% of the time, Pallas kernels for 0%

commit v1 on v0

--- a/solution.py
+++ b/solution.py
@@ -9,6 +9,9 @@
 ROW = ("row_0", "row_1", "row_2")
 COL = ("col_0", "col_1")
 ROW_COL = ("row_0", "row_1", "row_2", "col_0", "col_1")
+attach_sizes = lambda xx, net_axis: jnp.concatenate(
+    lax.all_to_all(jnp.stack(lax.axis_size(net_axis) * [xx], axis=0), net_axis, 0, 0), axis=0
+)
 
 
 def piece_ends(length, count):
@@ -19,7 +22,7 @@
 def all_blocks(x, axes, order):
     tiles = x[None]
     for k in order:
-        tiles = lax.all_gather(tiles, axes[k], axis=0, tiled=True)
+        tiles = attach_sizes(tiles, axes[k])
     held = [lax.axis_size(axes[k]) for k in reversed(order)]
     tiles = tiles.reshape(*held, *x.shape)
     turned = sorted(range(len(order)), key=lambda place: order[len(order) - 1 - place])

time: 406 us -> 496 us (1.22)
  waiting for transfers between devices: 135 us -> 220 us
  blocking collectives: 130 us -> 68.7 us
  starting transfers between devices: 0.21 us -> 59.1 us
  other arithmetic: 14.7 us -> 20.8 us
    all_to_all x0 -> x14, waiting for transfers between devices: none -> 131 us  [lax.all_to_all(jnp.stack(lax.axis_size(net_axis) * [xx], axis=0), net_axi...]
    all_gather x16 -> x0, blocking collectives: 130 us -> none  [all_blocks(): tiles = lax.all_gather(tiles, axes[k], axis=0, tiled=True)]
    all_to_all x0 -> x6, blocking collectives: none -> 68.7 us  [lax.all_to_all(jnp.stack(lax.axis_size(net_axis) * [xx], axis=0), net_axi...]
    all_to_all x0 -> x14, starting transfers between devices: none -> 58.7 us  [lax.all_to_all(jnp.stack(lax.axis_size(net_axis) * [xx], axis=0), net_axi...]
    all_gather x1, waiting for transfers between devices: 38.9 us -> 0.02 us  [per_device(): left_full = lax.all_gather(chosen_left, COL, axis=3, tiled=True)]
    reshape x3 -> x0, local copies, waits for them, and re-layouts: 12.2 us -> none  [all_blocks(): tiles.transpose(*turned, *range(len(order), tiles.ndim))]
    another operation x0 -> x10, local copies, waits for them, and re-layouts: none -> 9.92 us  [the longest x9 7.94 us: jnp.stack(lax.axis_size(net_axis) * [xx], axis=0)]
    another operation x0 -> x12, other arithmetic: none -> 8.09 us  [jnp.stack(lax.axis_size(net_axis) * [xx], axis=0)]
  transfers between devices with their start and end apart: 6 -> 16, of which waited for: 3 -> 15; matrix products, arithmetic and copies ran while one was open for 16% -> 13% of each run, Pallas kernels for 0% -> 0%
where the time goes in v1:
time: 496 us; the launch traced here: 489 us
  waiting for transfers between devices  220 us (44%)
  blocking collectives  68.7 us (14%)
  matrix products  68.2 us (14%)
  starting transfers between devices  59.1 us (12%)
  local copies, waits for them, and re-layouts  37.6 us (8%)
  other arithmetic  20.8 us (4%)
  between operations  14.7 us (3%)
    all_to_all x14, waiting for transfers between devices, lax.all_to_all(jnp.stack(lax.axis_size(net_axis) * [xx], axis=0), net_axi...  131 us
    all_gather x1, waiting for transfers between devices, per_device(): lax.all_gather(vertex_right, ROW, axis=4, tiled=True)  88.4 us
    all_to_all x6, blocking collectives, lax.all_to_all(jnp.stack(lax.axis_size(net_axis) * [xx], axis=0), net_axi...  68.7 us
    all_to_all x14, starting transfers between devices, lax.all_to_all(jnp.stack(lax.axis_size(net_axis) * [xx], axis=0), net_axi...  58.7 us
    dot_general x3, matrix products, complex_product(): jnp.matmul(first_im, second_re, precision=highest)  17 us
    unnamed x4, matrix products  16.6 us
    dot_general x3, matrix products, complex_product(): jnp.matmul(first_re, second_re, precision=highest)  12.2 us
    dot_general x3, matrix products, complex_product(): jnp.matmul(first_re, second_im, precision=highest)  11.3 us
  transfers between devices with their start and end apart: 16, of which 15 were waited for; matrix products, arithmetic and copies ran while one was open for 13% of the time, Pallas kernels for 0%

profile of v1, /device:TPU:1, one launch (start us, length us, event | category | flops | bytes accessed | tf_op | source)
XLA Modules:
  0.0 488.8 jit_solution(10570629052708044330)
XLA Ops:
  14.5 4.6 all-to-all-start.5
  26.2 4.3 all-to-all-start
  30.5 58.7 %all-to-all-done = f32[2,1,3,2,1,512]{5,4,3,2,1,0:T(1,128)S(1)} async-done(((f32[2,1,3,2,1,512]{5,4,3,2,1,0:T(1,128)}), f32[2,1,3,2,1,512]{5,4,3,2,1,0:T(1,128)S(1)}, u32[]{:S(2)}, u32[]{:S(2)}) %all-to-all-start) | async-done | bytes 24608 | tf_op jit(solution)/shard_map/all_to_all | solution.py:13
  89.2 3.9 all_to_all.100
  96.4 4.4 all-to-all-done.6
  101.4 9.4 %all-to-all-start.15 = ((f32[4,1,3,2,1,512]{5,3,2,4,1,0:T(2,128)}), f32[4,1,3,2,1,512]{5,3,2,4,1,0:T(2,128)S(1)}, u32[]{:S(2)}, u32[]{:S(2)}) async-start(f32[4,1,3,2,1,512]{5,3,2,4,1,0:T(2,128)} %stack.111), calls=%async_computation.15 | async-start | bytes 98304 | tf_op jit(solution)/shard_map/all_to_all | solution.py:13
  119.2 4.0 all-to-all-done.12
  130.3 5.5 %all-to-all-start.1 = ((f32[4,2,3,2,1,512]{5,3,2,1,4,0:T(2,128)}), f32[4,2,3,2,1,512]{5,3,2,1,4,0:T(2,128)S(1)}, u32[]{:S(2)}, u32[]{:S(2)}) async-start(f32[4,2,3,2,1,512]{5,3,2,1,4,0:T(2,128)} %stack.97), calls=%async_computation.1 | async-start | bytes 196608 | tf_op jit(solution)/shard_map/all_to_all | solution.py:13
  135.9 4.6 all-to-all-done.1
  140.5 9.9 %all_to_all.101 = f32[2,8,3,2,1,512]{5,3,2,1,4,0:T(2,128)S(1)} all-to-all(f32[2,8,3,2,1,512]{5,3,2,1,4,0:T(2,128)S(1)} %pad_maximum_fusion.5), channel_id=1, replica_groups=mesh['row_0'=4,'row_1'=2,'row_2'=2,'col_0'=2,'col_1'=4] {'row_2'}, dimensions={0} | all-to-all | bytes 393216 | tf_op jit(solution)/shard_map/all_to_all | solution.py:13
  154.6 5.2 %all-to-all-done.7 = f32[4,4,3,2,1,512]{5,3,2,1,4,0:T(2,128)S(1)} async-done(((f32[4,4,3,2,1,512]{5,3,2,1,4,0:T(2,128)}), f32[4,4,3,2,1,512]{5,3,2,1,4,0:T(2,128)S(1)}, u32[]{:S(2)}, u32[]{:S(2)}) %all-to-all-start.7) | async-done | bytes 196640 | tf_op jit(solution)/shard_map/all_to_all | solution.py:13
  159.9 9.0 %all_to_all.102 = f32[2,16,3,2,1,512]{5,3,2,1,4,0:T(2,128)S(1)} all-to-all(f32[2,16,3,2,1,512]{5,3,2,1,4,0:T(2,128)S(1)} %pad_maximum_fusion.4), channel_id=1, replica_groups=mesh['row_0'=4,'row_1'=2,'row_2'=2,'col_0'=2,'col_1'=4] {'row_1'}, dimensions={0} | all-to-all | bytes 786432 | tf_op jit(solution)/shard_map/all_to_all | solution.py:13
  173.3 6.1 %all-to-all-done.2 = f32[4,8,3,2,1,512]{5,3,2,1,4,0:T(2,128)S(1)} async-done(((f32[4,8,3,2,1,512]{5,3,2,1,4,0:T(2,128)}), f32[4,8,3,2,1,512]{5,3,2,1,4,0:T(2,128)S(1)}, u32[]{:S(2)}, u32[]{:S(2)}) %all-to-all-start.2) | async-done | bytes 393248 | tf_op jit(solution)/shard_map/all_to_all | solution.py:13
  184.0 5.9 %all-to-all-done.13 = f32[4,8,3,2,1,512]{5,3,2,1,4,0:T(2,128)S(1)} async-done(((f32[4,8,3,2,1,512]{5,3,2,1,4,0:T(2,128)}), f32[4,8,3,2,1,512]{5,3,2,1,4,0:T(2,128)S(1)}, u32[]{:S(2)}, u32[]{:S(2)}) %all-to-all-start.13) | async-done | bytes 393248 | tf_op jit(solution)/shard_map/all_to_all | solution.py:13
  190.0 10.0 %all_to_all.103 = f32[2,32,3,2,1,512]{5,3,2,1,4,0:T(2,128)} all-to-all(f32[2,32,3,2,1,512]{5,3,2,1,4,0:T(2,128)S(1)} %pad_maximum_fusion.2), channel_id=1, replica_groups=mesh['row_0'=4,'row_1'=2,'row_2'=2,'col_0'=2,'col_1'=4] {'col_0'}, dimensions={0} | all-to-all | bytes 1572864 | tf_op jit(solution)/shard_map/all_to_all | solution.py:13
  206.7 6.2 %all-to-all-done.8 = f32[4,16,3,2,1,512]{5,3,2,1,4,0:T(2,128)S(1)} async-done(((f32[4,16,3,2,1,512]{5,3,2,1,4,0:T(2,128)}), f32[4,16,3,2,1,512]{5,3,2,1,4,0:T(2,128)S(1)}, u32[]{:S(2)}, u32[]{:S(2)}) %all-to-all-start.8) | async-done | bytes 786464 | tf_op jit(solution)/shard_map/all_to_all | solution.py:13
  212.8 12.5 %all_to_all.104 = f32[2,64,3,2,1,512]{5,3,2,1,4,0:T(2,128)} all-to-all(f32[2,64,3,2,1,512]{5,3,2,1,4,0:T(2,128)S(1)} %pad_maximum_fusion), channel_id=1, replica_groups=mesh['row_0'=4,'row_1'=2,'row_2'=2,'col_0'=2,'col_1'=4] {'row_2'}, dimensions={0} | all-to-all | bytes 3145728 | tf_op jit(solution)/shard_map/all_to_all | solution.py:13
  232.1 18.8 %all-to-all-done.14 = f32[4,32,3,2,1,512]{5,3,2,1,4,0:T(2,128)S(1)} async-done(((f32[4,32,3,2,1,512]{5,3,2,1,4,0:T(2,128)}), f32[4,32,3,2,1,512]{5,3,2,1,4,0:T(2,128)S(1)}, u32[]{:S(2)}, u32[]{:S(2)}) %all-to-all-start.14) | async-done | bytes 1572896 | tf_op jit(solution)/shard_map/all_to_all | solution.py:13
  250.8 23.4 %all_to_all.105 = f32[2,64,3,2,1,512]{5,3,2,1,4,0:T(2,128)} all-to-all(f32[2,64,3,2,1,512]{5,3,2,1,4,0:T(2,128)} %pad_maximum_fusion.1), channel_id=1, replica_groups=mesh['row_0'=4,'row_1'=2,'row_2'=2,'col_0'=2,'col_1'=4] {'col_0'}, dimensions={0} | all-to-all | bytes 3145728 | tf_op jit(solution)/shard_map/all_to_all | solution.py:13
  275.8 4.3 all-to-all-start.19
  290.2 8.7 %all-to-all-done.19 = f32[4,32,3,2,1,512]{5,3,2,1,4,0:T(2,128)} async-done(((f32[4,32,3,2,1,512]{5,3,2,1,4,0:T(2,128)}), f32[4,32,3,2,1,512]{5,3,2,1,4,0:T(2,128)}, u32[]{:S(2)}, u32[]{:S(2)}) %all-to-all-start.19) | async-done | bytes 1572896 | tf_op jit(solution)/shard_map/all_to_all | solution.py:13
  298.9 6.0 %maximum_bitcast_fusion = f32[3,2,128,4,512]{4,1,0,2,3:T(2,128)S(1)} fusion(f32[128,3,2,1,512]{4,2,1,0,3:T(2,128)} %bitcast.31, f32[128,3,2,1,512]{4,2,1,0,3:T(2,128)} %bitcast.191, f32[128,3,2,1,512]{4,2,1,0,3:T(2,128)} %bitcast.192, f32[128,3,2,1,512]{4,2,1,0,3:T(2,128)} %bitcast.190), kind=kLoop, calls=%fused_computation.3 | loop fusion | flops 4718592 | bytes 12582912 | tf_op jit(solution)/shard_map/transpose | solution.py:35
  304.9 6.7 %copy.57 = f32[3,2,128,4,512]{4,3,2,0,1:T(4,128)} copy(f32[3,2,128,4,512]{4,1,0,2,3:T(2,128)S(1)} %maximum_bitcast_fusion) | data formatting | bytes 12582912 | tf_op jit(solution)/shard_map/transpose | solution.py:35
  311.6 8.2 %broadcast_in_dim_reshape.3 = f32[3,1,2,512,512]{4,3,0,2,1:T(8,128)} reshape(f32[3,2,128,4,512]{4,3,2,0,1:T(4,128)} %copy.57) | data formatting | bytes 12582912 | tf_op jit(solution)/shard_map/broadcast_in_dim;reshape | solution.py:87
  319.8 5.2 %fusion.3 = f32[3,512,64]{1,2,0:S(1)} fusion(f32[3,512,64]{1,2,0:T(8,128)S(1)} %bitcast.195, f32[3,1,2,512,512]{4,3,0,2,1:T(8,128)} %broadcast_in_dim_reshape.3), kind=kOutput, calls=%fused_computation.10 | convolution fusion | flops 603979776 | bytes 3932160
  325.0 5.0 %fusion.2 = f32[3,512,64]{1,2,0:S(1)} fusion(f32[3,512,64]{1,2,0:T(8,128)S(1)} %bitcast.196, f32[3,1,2,512,512]{4,3,0,2,1:T(8,128)} %broadcast_in_dim_reshape.3), kind=kOutput, calls=%fused_computation.9 | convolution fusion | flops 603979776 | bytes 3932160
  337.5 88.4 %all-gather.5.cloned.1.call-done = f32[3,2,2,512,512]{3,4,1,0,2:T(8,128)} async-done(((f32[3,2,2,512,32]{3,4,1,0,2:T(8,128)}), f32[3,2,2,512,512]{3,4,1,0,2:T(8,128)}) %all-gather.5.cloned.1.call-update) | async-done | bytes 12582928 | tf_op jit(solution)/shard_map/all_gather | solution.py:88
  426.0 5.8 %fusion.13 = f32[512,2,512]{2,0,1:T(8,128)S(1)} fusion(f32[3,2,2,512,512]{3,4,1,0,2:T(8,128)} %all-gather.5.cloned.1.call-done, f32[1,3,2,512,512]{4,3,2,1,0:T(8,128)} %all-gather.3.cloned.1.call-done), kind=kOutput, calls=%fused_computation.32 | convolution fusion | flops 3221225472 | bytes 5242880 | tf_op jit(solution)/shard_map/dot_general | solution.py:55
  431.8 5.5 %fusion.9 = f32[512,2,512]{2,0,1:T(8,128)S(1)} fusion(f32[3,2,2,512,512]{3,4,1,0,2:T(8,128)} %all-gather.5.cloned.1.call-done, f32[1,3,2,512,512]{4,3,2,1,0:T(8,128)} %all-gather.3.cloned.1.call-done), kind=kOutput, calls=%fused_computation.28 | convolution fusion | flops 3221225472 | bytes 5242880 | tf_op jit(solution)/shard_map/dot_general | solution.py:55
  437.3 5.6 %fusion.5 = f32[512,2,512]{2,0,1:T(8,128)S(1)} fusion(f32[3,2,2,512,512]{3,4,1,0,2:T(8,128)} %all-gather.5.cloned.1.call-done, f32[1,3,2,512,512]{4,3,2,1,0:T(8,128)} %all-gather.3.cloned.1.call-done), kind=kOutput, calls=%fused_computation.24 | convolution fusion | flops 3221225472 | bytes 5242880 | tf_op jit(solution)/shard_map/dot_general | solution.py:55
  443.0 5.1 %fusion.14 = f32[512,2,512]{2,0,1:T(8,128)S(1)} fusion(f32[3,2,2,512,512]{3,4,1,0,2:T(8,128)S(1)} %copy-done.3, f32[1,3,2,512,512]{4,3,2,1,0:T(8,128)} %all-gather.3.cloned.1.call-done), kind=kOutput, calls=%fused_computation.33 | convolution fusion | flops 3221225472 | bytes 5242880 | tf_op jit(solution)/shard_map/dot_general | solution.py:52
  458.9 4.0 add_bitcast_fusion.1
  (91 shorter events, 109.0 us)
Async XLA Ops:
  6.5 4.1 copy-start
  6.5 331.0 %all-gather.3.cloned.1.call-start = ((), (), s32[]{:S(2)}) async-start(), calls=%async_computation.20 | async-start | bytes 7077888 | tf_op jit(solution)/shard_map/all_gather | solution.py:86
  14.5 5.7 %all-to-all-start.5 = ((f32[2,1,3,2,1,512]{5,4,3,2,1,0:T(1,128)}), f32[2,1,3,2,1,512]{5,4,3,2,1,0:T(1,128)S(1)}, u32[]{:S(2)}, u32[]{:S(2)}) async-start(f32[2,1,3,2,1,512]{5,4,3,2,1,0:T(1,128)} %pad_maximum_fusion.11), calls=%async_computation.5 | async-start | bytes 49152 | tf_op jit(solution)/shard_map/all_to_all | solution.py:13
  20.2 6.0 %all-to-all-start.10 = ((f32[2,1,3,2,1,512]{5,4,3,2,1,0:T(1,128)}), f32[2,1,3,2,1,512]{5,4,3,2,1,0:T(1,128)S(1)}, u32[]{:S(2)}, u32[]{:S(2)}) async-start(f32[2,1,3,2,1,512]{5,4,3,2,1,0:T(1,128)} %pad_maximum_fusion.12), calls=%async_computation.10 | async-start | bytes 49152 | tf_op jit(solution)/shard_map/all_to_all | solution.py:13
  26.2 63.0 %all-to-all-start = ((f32[2,1,3,2,1,512]{5,4,3,2,1,0:T(1,128)}), f32[2,1,3,2,1,512]{5,4,3,2,1,0:T(1,128)S(1)}, u32[]{:S(2)}, u32[]{:S(2)}) async-start(f32[2,1,3,2,1,512]{5,4,3,2,1,0:T(1,128)} %pad_maximum_fusion.10), calls=%async_computation | async-start | bytes 49152 | tf_op jit(solution)/shard_map/all_to_all | solution.py:13
  93.1 7.7 %all-to-all-start.6 = ((f32[2,2,3,2,1,512]{5,4,3,2,1,0:T(1,128)}), f32[2,2,3,2,1,512]{5,4,3,2,1,0:T(1,128)S(1)}, u32[]{:S(2)}, u32[]{:S(2)}) async-start(f32[2,2,3,2,1,512]{5,4,3,2,1,0:T(1,128)} %pad_maximum_fusion.8), calls=%async_computation.6 | async-start | bytes 98304 | tf_op jit(solution)/shard_map/all_to_all | solution.py:13
  101.4 13.8 %all-to-all-start.15 = ((f32[4,1,3,2,1,512]{5,3,2,4,1,0:T(2,128)}), f32[4,1,3,2,1,512]{5,3,2,4,1,0:T(2,128)S(1)}, u32[]{:S(2)}, u32[]{:S(2)}) async-start(f32[4,1,3,2,1,512]{5,3,2,4,1,0:T(2,128)} %stack.111), calls=%async_computation.15 | async-start | bytes 98304 | tf_op jit(solution)/shard_map/all_to_all | solution.py:13
  115.2 8.0 %all-to-all-start.12 = ((f32[2,4,3,2,1,512]{5,4,3,2,1,0:T(1,128)}), f32[2,4,3,2,1,512]{5,4,3,2,1,0:T(1,128)S(1)}, u32[]{:S(2)}, u32[]{:S(2)}) async-start(f32[2,4,3,2,1,512]{5,4,3,2,1,0:T(1,128)} %pad_maximum_fusion.6), calls=%async_computation.12 | async-start | bytes 196608 | tf_op jit(solution)/shard_map/all_to_all | solution.py:13
  123.2 6.5 %all-to-all-start.16 = ((f32[2,4,3,2,1,512]{5,3,2,1,4,0:T(2,128)}), f32[2,4,3,2,1,512]{5,3,2,1,4,0:T(2,128)S(1)}, u32[]{:S(2)}, u32[]{:S(2)}) async-start(f32[2,4,3,2,1,512]{5,3,2,1,4,0:T(2,128)} %pad_maximum_fusion.7), calls=%async_computation.16 | async-start | bytes 196608 | tf_op jit(solution)/shard_map/all_to_all | solution.py:13
  130.3 10.2 %all-to-all-start.1 = ((f32[4,2,3,2,1,512]{5,3,2,1,4,0:T(2,128)}), f32[4,2,3,2,1,512]{5,3,2,1,4,0:T(2,128)S(1)}, u32[]{:S(2)}, u32[]{:S(2)}) async-start(f32[4,2,3,2,1,512]{5,3,2,1,4,0:T(2,128)} %stack.97), calls=%async_computation.1 | async-start | bytes 196608 | tf_op jit(solution)/shard_map/all_to_all | solution.py:13
  151.1 8.7 %all-to-all-start.7 = ((f32[4,4,3,2,1,512]{5,3,2,1,4,0:T(2,128)}), f32[4,4,3,2,1,512]{5,3,2,1,4,0:T(2,128)S(1)}, u32[]{:S(2)}, u32[]{:S(2)}) async-start(f32[4,4,3,2,1,512]{5,3,2,1,4,0:T(2,128)} %stack.103), calls=%async_computation.7 | async-start | bytes 393216 | tf_op jit(solution)/shard_map/all_to_all | solution.py:13
  169.8 9.7 %all-to-all-start.2 = ((f32[4,8,3,2,1,512]{5,3,2,1,4,0:T(2,128)}), f32[4,8,3,2,1,512]{5,3,2,1,4,0:T(2,128)S(1)}, u32[]{:S(2)}, u32[]{:S(2)}) async-start(f32[4,8,3,2,1,512]{5,3,2,1,4,0:T(2,128)} %stack.98), calls=%async_computation.2 | async-start | bytes 786432 | tf_op jit(solution)/shard_map/all_to_all | solution.py:13
  180.3 9.7 %all-to-all-start.13 = ((f32[4,8,3,2,1,512]{5,3,2,1,4,0:T(2,128)}), f32[4,8,3,2,1,512]{5,3,2,1,4,0:T(2,128)S(1)}, u32[]{:S(2)}, u32[]{:S(2)}) async-start(f32[4,8,3,2,1,512]{5,3,2,1,4,0:T(2,128)} %stack.109), calls=%async_computation.13 | async-start | bytes 786432 | tf_op jit(solution)/shard_map/all_to_all | solution.py:13
  201.0 11.8 %all-to-all-start.8 = ((f32[4,16,3,2,1,512]{5,3,2,1,4,0:T(2,128)}), f32[4,16,3,2,1,512]{5,3,2,1,4,0:T(2,128)S(1)}, u32[]{:S(2)}, u32[]{:S(2)}) async-start(f32[4,16,3,2,1,512]{5,3,2,1,4,0:T(2,128)} %stack.104), calls=%async_computation.8 | async-start | bytes 1572864 | tf_op jit(solution)/shard_map/all_to_all | solution.py:13
  226.9 24.0 %all-to-all-start.14 = ((f32[4,32,3,2,1,512]{5,3,2,1,4,0:T(2,128)}), f32[4,32,3,2,1,512]{5,3,2,1,4,0:T(2,128)S(1)}, u32[]{:S(2)}, u32[]{:S(2)}) async-start(f32[4,32,3,2,1,512]{5,3,2,1,4,0:T(2,128)} %stack.110), calls=%async_computation.14 | async-start | bytes 3145728 | tf_op jit(solution)/shard_map/all_to_all | solution.py:13
  250.8 24.9 %copy-start.6 = (f32[4,32,3,2,1,512]{5,3,2,1,4,0:T(2,128)}, f32[4,32,3,2,1,512]{5,3,2,1,4,0:T(2,128)S(1)}, u32[]{:S(2)}) copy-start(f32[4,32,3,2,1,512]{5,3,2,1,4,0:T(2,128)S(1)} %all-to-all-done.14) | copy-start | bytes 4718596
  275.8 23.1 %all-to-all-start.19 = ((f32[4,32,3,2,1,512]{5,3,2,1,4,0:T(2,128)}), f32[4,32,3,2,1,512]{5,3,2,1,4,0:T(2,128)}, u32[]{:S(2)}, u32[]{:S(2)}) async-start(f32[4,32,3,2,1,512]{5,3,2,1,4,0:T(2,128)} %stack.115), calls=%async_computation.19 | async-start | bytes 3145728 | tf_op jit(solution)/shard_map/all_to_all | solution.py:13
  280.1 145.8 %all-gather.5.cloned.1.call-start = ((), (), s32[]{:S(2)}) async-start(), calls=%async_computation.21 | async-start | bytes 13369344 | tf_op jit(solution)/shard_map/all_gather | solution.py:88
  282.7 1.4 copy-start.5
  283.5 2.6 copy-start.7
  284.1 4.1 copy-start.8
  319.8 10.2 %copy-start.2 = (f32[3,1,2,512,512]{4,3,0,2,1:T(8,128)S(1)}, f32[3,1,2,512,512]{4,3,0,2,1:T(8,128)}, u32[]{:S(2)}) copy-start(f32[3,1,2,512,512]{4,3,0,2,1:T(8,128)} %broadcast_in_dim_reshape.3) | copy-start | bytes 18874372
  426.0 17.0 %copy-start.3 = (f32[3,2,2,512,512]{3,4,1,0,2:T(8,128)S(1)}, f32[3,2,2,512,512]{3,4,1,0,2:T(8,128)}, u32[]{:S(2)}) copy-start(f32[3,2,2,512,512]{3,4,1,0,2:T(8,128)} %all-gather.5.cloned.1.call-done) | copy-start | bytes 37748740
  437.3 10.7 %copy-start.4 = (f32[1,3,2,512,512]{4,3,2,1,0:T(8,128)S(1)}, f32[1,3,2,512,512]{4,3,2,1,0:T(8,128)}, u32[]{:S(2)}) copy-start(f32[1,3,2,512,512]{4,3,2,1,0:T(8,128)} %all-gather.3.cloned.1.call-done) | copy-start | bytes 18874372
  477.7 4.1 copy-start.1
Sparse Core Ops, SparseCore 0:
  12.4 75.2 all-gather.2
  337.6 88.3 all-gather.4
